TPU v7x, 32 devices: a whole 2x2x4 slice. The times are simulated.
32 devices in a mesh: band: 16 (over z, y, core), grid: 2 (over x).
Axes of the slice: x: 2, y: 2, z: 4, core: 2. Of those that a mesh axis runs over, the one named last changes fastest.
Arguments:
- bands: float32 [32, 72, 5184], P('band', 'grid'), may hold values from -2.4 to 2.4
Outputs:
- exchange_terms: float32 [32, 72, 5184], P('band', 'grid')
All inputs are finite; a program needn't handle non-finite values.
Results may differ from a plain program's by a relative error of at most 0.0001.
Values sent between devices are 32-bit elements; how exact they have to be, the bound alone decides.
No kernel may reach another device: no remote copies, remote signals or barrier semaphores. Data moves between devices by JAX's collectives and lax.ppermute only.
A program may use at most 128 MiB of HBM per device.

v0:
```python
import math

import jax
import jax.numpy as jnp
from jax import lax
from jax.sharding import PartitionSpec as P

GRID = 72
STEPS = 3


spacing = 0.5167


def shifted(value, axis, steps):
    count = lax.axis_size(axis)
    pairs = [(source, (source + steps) % count) for source in range(count)]
    return lax.ppermute(value, axis, pairs)


def tables(count):
    index = jnp.arange(count, dtype=jnp.int32)
    half = count // 2
    freq = jnp.where(index <= half, index, index - half)
    phase = (freq[:, None] * index[None, :] % count).astype(jnp.float32) * (2.0 * math.pi / count)
    table = jnp.where(index[:, None] <= half, jnp.cos(phase), jnp.sin(phase))
    weight = jnp.where((index == 0) | (index == half), 1.0, 2.0).astype(jnp.float32)
    square = freq.astype(jnp.float32) ** 2
    factor = (2.0 * math.pi / (count * spacing)) ** 2
    ksq = factor * (square[:, None, None] + square[None, :, None] + square[None, None, :])
    safe = jnp.where(ksq > 0, ksq, 1.0)
    coulomb = jnp.where(ksq > 0, 4.0 * math.pi / safe, 0.0)
    weights = weight[:, None, None] * weight[None, :, None] * weight[None, None, :]
    kernel = coulomb * weights / float(count**3)
    return (table, kernel.reshape(count, count * count))


def forward_axis(values, table):
    return jnp.einsum("pmc,kc->pkm", values, table, precision=lax.Precision.HIGHEST)


def inverse_axis(values, table):
    return jnp.einsum("pmk,kr->prm", values, table, precision=lax.Precision.HIGHEST)


def coulomb_filter(density, table, kernel):
    count = table.shape[0]
    pairs = density.shape[0]
    work = forward_axis(density.reshape(pairs, count * count, count), table)
    work = forward_axis(work.reshape(pairs, count * count, count), table)
    work = forward_axis(work.reshape(pairs, count * count, count), table)
    work = work * kernel[None]
    work = inverse_axis(work.reshape(pairs, count * count, count), table)
    work = inverse_axis(work.reshape(pairs, count * count, count), table)
    work = inverse_axis(work.reshape(pairs, count * count, count), table)
    return work


def pair_terms(home, visit, table, kernel):
    home_count = home.shape[0]
    visit_count = visit.shape[0]
    count = home.shape[1]
    density = (home[:, None] * visit[None]).reshape(home_count * visit_count, count, home.shape[2])
    potential = coulomb_filter(density, table, kernel).reshape(
        home_count, visit_count, count, home.shape[2]
    )
    home_part = -jnp.sum(potential * visit[None], axis=1)
    partner = -jnp.sum(potential * home[:, None], axis=0)
    return (home_part, partner)


def local(bands):
    table, kernel = tables(GRID)
    whole = lax.all_gather(bands, "grid", axis=1, tiled=True)
    share = whole.shape[0] // lax.axis_size("grid")
    first = lax.axis_index("grid") * share
    visit = lax.dynamic_slice_in_dim(whole, first, share, 0)
    home_total = jnp.zeros_like(whole)
    carried = jnp.zeros_like(visit)
    for step in range(STEPS):
        visit = shifted(visit, "band", 1)
        home_part, partner = pair_terms(whole, visit, table, kernel)
        home_total = home_total + home_part
        carried = carried + partner
        if step + 1 < STEPS:
            carried = shifted(carried, "band", 1)
    returned = shifted(carried, "band", -STEPS)
    own_rows = lax.dynamic_slice_in_dim(home_total, first, share, 0) + returned
    home_total = lax.dynamic_update_slice_in_dim(home_total, own_rows, first, 0)
    return lax.psum_scatter(home_total, "grid", scatter_dimension=1, tiled=True)


def solution(mesh):
    return jax.shard_map(
        local,
        mesh=mesh,
        in_specs=(P("band", "grid", None),),
        out_specs=P("band", "grid", None),
        check_vma=False,
    )
```

profile of v0, /device:TPU:0, one launch (start us, length us, event | category | flops | bytes accessed | tf_op | source)
XLA Modules:
  0.0 573.2 jit_solution(4866386390769388456)
XLA Ops:
  7.3 47.8 %all-gather.2.cloned.1.call-done = f32[2,72,5184]{2,0,1:T(2,128)} async-done(((f32[2,36,5184]{2,0,1:T(2,128)}), f32[2,72,5184]{2,0,1:T(2,128)}) %all-gather.2.cloned.1.call-update) | async-done | bytes 2986000 | tf_op jit(solution)/shard_map/all_gather | solution.py:74
  58.4 21.9 %collective-permute-done = f32[1,72,5184]{2,0,1:T(1,128)S(1)} collective-permute-done((f32[1,72,5184]{2,0,1:T(1,128)S(1)}, f32[1,72,5184]{2,0,1:T(1,128)S(1)}, u32[]{:S(2)}, u32[]{:S(2)}) %collective-permute-start) | collective-permute-done | bytes 1493024 | tf_op jit(solution)/shard_map/ppermute | solution.py:18
  80.4 21.8 %collective-permute-done.1 = f32[1,72,5184]{2,0,1:T(1,128)} collective-permute-done((f32[1,72,5184]{2,0,1:T(1,128)S(1)}, f32[1,72,5184]{2,0,1:T(1,128)}, u32[]{:S(2)}, u32[]{:S(2)}) %collective-permute-start.1) | collective-permute-done | bytes 1493024 | tf_op jit(solution)/shard_map/ppermute | solution.py:18
  112.6 11.8 %collective-permute-done.2 = f32[1,72,5184]{2,0,1:T(1,128)} collective-permute-done((f32[1,72,5184]{2,0,1:T(1,128)}, f32[1,72,5184]{2,0,1:T(1,128)}, u32[]{:S(2)}, u32[]{:S(2)}) %collective-permute-start.2) | collective-permute-done | bytes 1493024 | tf_op jit(solution)/shard_map/ppermute | solution.py:18
  136.3 9.4 %convolution_bitcast_fusion.9 = f32[2,72,5184]{2,1,0:T(8,128)} fusion(f32[2,5184,72]{2,1,0:T(8,128)} %reshape_reshape.10, s32[72]{0:T(128)S(1)} %add_select_fusion.1, pred[72]{0:T(512)(128)(4,1)S(1)} %iota_compare_fusion), kind=kOutput, calls=%fused_computation.15 | convolution fusion | flops 645024384 | bytes 5972328 | tf_op jit(solution)/shard_map/pmc,kc->pkm/dot_general | solution.py:39
  151.6 9.4 %convolution_bitcast_fusion.8 = f32[2,72,5184]{2,1,0:T(8,128)} fusion(f32[2,5184,72]{2,1,0:T(8,128)} %reshape.285, s32[72]{0:T(128)S(1)} %add_select_fusion.1, pred[72]{0:T(512)(128)(4,1)S(1)} %iota_compare_fusion), kind=kOutput, calls=%fused_computation.14 | convolution fusion | flops 645024384 | bytes 5972328 | tf_op jit(solution)/shard_map/pmc,kc->pkm/dot_general | solution.py:39
  167.0 9.4 %fusion.1 = f32[2,72,5184]{2,1,0:T(8,128)} fusion(f32[2,5184,72]{2,1,0:T(8,128)} %reshape.286, f32[72,5184]{1,0:T(8,128)S(1)} %fusion.5, s32[72]{0:T(128)S(1)} %add_select_fusion.1, pred[72]{0:T(512)(128)(4,1)S(1)} %iota_compare_fusion), kind=kOutput, calls=%fused_computation.4 | convolution fusion | flops 645770880 | bytes 7465320 | tf_op jit(solution)/shard_map/pmc,kc->pkm/dot_general | solution.py:39
  182.3 9.7 %convolution_bitcast_fusion.7 = f32[2,72,5184]{2,1,0:T(8,128)} fusion(f32[2,5184,72]{2,1,0:T(8,128)} %reshape.287, s32[72]{0:T(128)S(1)} %add_select_fusion.1, pred[72]{0:T(512)(128)(4,1)S(1)} %iota_compare_fusion), kind=kOutput, calls=%fused_computation.13 | convolution fusion | flops 645024384 | bytes 5972328 | tf_op jit(solution)/shard_map/pmk,kr->prm/dot_general | solution.py:43
  198.0 9.7 %convolution_bitcast_fusion.6 = f32[2,72,5184]{2,1,0:T(8,128)} fusion(f32[2,5184,72]{2,1,0:T(8,128)} %reshape.288, s32[72]{0:T(128)S(1)} %add_select_fusion.1, pred[72]{0:T(512)(128)(4,1)S(1)} %iota_compare_fusion), kind=kOutput, calls=%fused_computation.12 | convolution fusion | flops 645024384 | bytes 5972328 | tf_op jit(solution)/shard_map/pmk,kr->prm/dot_general | solution.py:43
  213.5 9.7 %convolution_bitcast_fusion.5 = f32[2,72,5184]{2,1,0:T(8,128)} fusion(f32[2,5184,72]{2,1,0:T(8,128)} %reshape.289, s32[72]{0:T(128)S(1)} %add_select_fusion.1, pred[72]{0:T(512)(128)(4,1)S(1)} %iota_compare_fusion), kind=kOutput, calls=%fused_computation.11 | convolution fusion | flops 645024384 | bytes 5972328 | tf_op jit(solution)/shard_map/pmk,kr->prm/dot_general | solution.py:43
  244.6 9.3 %convolution_bitcast_fusion.13 = f32[2,72,5184]{2,1,0:T(8,128)} fusion(f32[2,5184,72]{2,1,0:T(8,128)} %reshape.280, s32[72]{0:T(128)S(1)} %add_select_fusion.1, pred[72]{0:T(512)(128)(4,1)S(1)} %iota_compare_fusion), kind=kOutput, calls=%fused_computation.19 | convolution fusion | flops 645024384 | bytes 5972328 | tf_op jit(solution)/shard_map/pmc,kc->pkm/dot_general | solution.py:39
  259.9 9.3 %fusion = f32[2,72,5184]{2,1,0:T(8,128)} fusion(f32[2,5184,72]{2,1,0:T(8,128)} %reshape.281, f32[72,5184]{1,0:T(8,128)S(1)} %fusion.5, s32[72]{0:T(128)S(1)} %add_select_fusion.1, pred[72]{0:T(512)(128)(4,1)S(1)} %iota_compare_fusion), kind=kOutput, calls=%fused_computation.3 | convolution fusion | flops 645770880 | bytes 7465320 | tf_op jit(solution)/shard_map/pmc,kc->pkm/dot_general | solution.py:39
  275.0 9.6 %convolution_bitcast_fusion.12 = f32[2,72,5184]{2,1,0:T(8,128)} fusion(f32[2,5184,72]{2,1,0:T(8,128)} %reshape.282, s32[72]{0:T(128)S(1)} %add_select_fusion.1, pred[72]{0:T(512)(128)(4,1)S(1)} %iota_compare_fusion), kind=kOutput, calls=%fused_computation.18 | convolution fusion | flops 645024384 | bytes 5972328 | tf_op jit(solution)/shard_map/pmk,kr->prm/dot_general | solution.py:43
  290.6 9.6 %convolution_bitcast_fusion.11 = f32[2,72,5184]{2,1,0:T(8,128)} fusion(f32[2,5184,72]{2,1,0:T(8,128)} %reshape.283, s32[72]{0:T(128)S(1)} %add_select_fusion.1, pred[72]{0:T(512)(128)(4,1)S(1)} %iota_compare_fusion), kind=kOutput, calls=%fused_computation.17 | convolution fusion | flops 645024384 | bytes 5972328 | tf_op jit(solution)/shard_map/pmk,kr->prm/dot_general | solution.py:43
  306.0 9.6 %convolution_bitcast_fusion.10 = f32[2,72,5184]{2,1,0:T(8,128)} fusion(f32[2,5184,72]{2,1,0:T(8,128)} %reshape.284, s32[72]{0:T(128)S(1)} %add_select_fusion.1, pred[72]{0:T(512)(128)(4,1)S(1)} %iota_compare_fusion), kind=kOutput, calls=%fused_computation.16 | convolution fusion | flops 645024384 | bytes 5972328 | tf_op jit(solution)/shard_map/pmk,kr->prm/dot_general | solution.py:43
  321.8 9.4 %convolution_bitcast_fusion.4 = f32[2,72,5184]{2,1,0:T(8,128)} fusion(f32[2,5184,72]{2,1,0:T(8,128)} %reshape_reshape.11, s32[72]{0:T(128)S(1)} %add_select_fusion.1, pred[72]{0:T(512)(128)(4,1)S(1)} %iota_compare_fusion), kind=kOutput, calls=%fused_computation.10 | convolution fusion | flops 645024384 | bytes 5972328 | tf_op jit(solution)/shard_map/pmc,kc->pkm/dot_general | solution.py:39
  337.1 9.4 %convolution_bitcast_fusion.3 = f32[2,72,5184]{2,1,0:T(8,128)} fusion(f32[2,5184,72]{2,1,0:T(8,128)} %reshape.290, s32[72]{0:T(128)S(1)} %add_select_fusion.1, pred[72]{0:T(512)(128)(4,1)S(1)} %iota_compare_fusion), kind=kOutput, calls=%fused_computation.9 | convolution fusion | flops 645024384 | bytes 5972328 | tf_op jit(solution)/shard_map/pmc,kc->pkm/dot_general | solution.py:39
  352.5 9.4 %fusion.2 = f32[2,72,5184]{2,1,0:T(8,128)} fusion(f32[2,5184,72]{2,1,0:T(8,128)} %reshape.291, f32[72,5184]{1,0:T(8,128)S(1)} %fusion.5, s32[72]{0:T(128)S(1)} %add_select_fusion.1, pred[72]{0:T(512)(128)(4,1)S(1)} %iota_compare_fusion), kind=kOutput, calls=%fused_computation.5 | convolution fusion | flops 645770880 | bytes 7465320 | tf_op jit(solution)/shard_map/pmc,kc->pkm/dot_general | solution.py:39
  380.2 9.7 %convolution_bitcast_fusion.1 = f32[2,72,5184]{2,1,0:T(8,128)} fusion(f32[2,5184,72]{2,1,0:T(8,128)} %reshape.293, s32[72]{0:T(128)S(1)} %add_select_fusion.1, pred[72]{0:T(512)(128)(4,1)S(1)} %iota_compare_fusion), kind=kOutput, calls=%fused_computation.7 | convolution fusion | flops 645024384 | bytes 5972328 | tf_op jit(solution)/shard_map/pmk,kr->prm/dot_general | solution.py:43
  396.2 13.0 %multiply_reduce_fusion = (f32[72,5184]{1,0:T(8,128)S(1)}, f32[72,5184]{1,0:T(8,128)S(1)}, f32[72,5184]{1,0:T(8,128)S(1)}, f32[2,72,5184]{2,1,0:T(8,128)S(1)}) fusion(f32[2,72,5184]{2,0,1:T(2,128)S(1)} %copy-done.1, f32[2,72,5184]{2,1,0:T(8,128)} %convolution_bitcast_fusion.10, f32[2,72,5184]{2,1,0:T(8,128)} %convolution_bitcast_fusion.5, ...), kind=kOutput, calls=%fused_computation.21 | convolution fusion | flops 654355584 | bytes 23888232 | tf_op jit(solution)/shard_map/pmk,kr->prm/dot_general | solution.py:43
  409.3 21.9 %collective-permute-done.3 = f32[1,72,5184]{2,1,0:T(8,128)S(1)} collective-permute-done((f32[1,72,5184]{2,1,0:T(8,128)S(1)}, f32[1,72,5184]{2,1,0:T(8,128)S(1)}, u32[]{:S(2)}, u32[]{:S(2)}) %collective-permute-start.3) | collective-permute-done | bytes 1493024 | tf_op jit(solution)/shard_map/ppermute | solution.py:18
  431.4 26.5 %collective-permute-done.4 = f32[1,72,5184]{2,1,0:T(8,128)S(1)} collective-permute-done((f32[1,72,5184]{2,1,0:T(8,128)S(1)}, f32[1,72,5184]{2,1,0:T(8,128)S(1)}, u32[]{:S(2)}, u32[]{:S(2)}) %collective-permute-start.4) | collective-permute-done | bytes 1493024 | tf_op jit(solution)/shard_map/ppermute | solution.py:18
  458.2 19.2 %collective-permute-done.5 = f32[1,72,5184]{2,1,0:T(8,128)S(1)} collective-permute-done((f32[1,72,5184]{2,1,0:T(8,128)S(1)}, f32[1,72,5184]{2,1,0:T(8,128)S(1)}, u32[]{:S(2)}, u32[]{:S(2)}) %collective-permute-start.5) | collective-permute-done | bytes 1493024 | tf_op jit(solution)/shard_map/ppermute | solution.py:18
  482.7 80.8 %all-reduce.3.cloned.1.call-done = f32[2,72,5184]{2,0,1:T(2,128)} async-done(((f32[2,72,5184]{2,0,1:T(2,128)}), f32[2,72,5184]{2,0,1:T(2,128)}) %all-reduce.3.cloned.1.call-update) | async-done | bytes 2986000
  (73 shorter events, 151.4 us)
Async XLA Ops:
  6.5 48.6 %all-gather.2.cloned.1.call-start = ((), (), s32[]{:S(2)}) async-start(), calls=%async_computation | async-start | bytes 4534272 | tf_op jit(solution)/shard_map/all_gather | solution.py:74
  7.3 556.3 %all-reduce.3.cloned.1.call-start = ((), (), s32[]{:S(2)}) async-start(), calls=%async_computation.1 | async-start | bytes 6045696
  58.3 21.9 %collective-permute-start = (f32[1,72,5184]{2,0,1:T(1,128)S(1)}, f32[1,72,5184]{2,0,1:T(1,128)S(1)}, u32[]{:S(2)}, u32[]{:S(2)}) collective-permute-start(f32[1,72,5184]{2,0,1:T(1,128)S(1)} %constant_dynamic-slice_fusion), channel_id=1, source_target_pairs={{0,2},{2,4},{4,6},{6,8},{8,10},{10,12},{12,14},{14,16},{16,18},{18... | collective-permute-start | bytes 4478984 | tf_op jit(solution)/shard_map/ppermute | solution.py:18
  80.2 22.0 %copy-start.5 = (f32[1,72,5184]{2,0,1:T(1,128)}, f32[1,72,5184]{2,0,1:T(1,128)S(1)}, u32[]{:S(2)}) copy-start(f32[1,72,5184]{2,0,1:T(1,128)S(1)} %collective-permute-done) | copy-start | bytes 4478980
  80.2 22.0 %collective-permute-start.1 = (f32[1,72,5184]{2,0,1:T(1,128)S(1)}, f32[1,72,5184]{2,0,1:T(1,128)}, u32[]{:S(2)}, u32[]{:S(2)}) collective-permute-start(f32[1,72,5184]{2,0,1:T(1,128)S(1)} %collective-permute-done), channel_id=1, source_target_pairs={{0,2},{2,4},{4,6},{6,8},{8,10},{10,12},{12,14},{14,16},{16,18},{18... | collective-permute-start | bytes 4478984 | tf_op jit(solution)/shard_map/ppermute | solution.py:18
  102.2 22.2 %collective-permute-start.2 = (f32[1,72,5184]{2,0,1:T(1,128)}, f32[1,72,5184]{2,0,1:T(1,128)}, u32[]{:S(2)}, u32[]{:S(2)}) collective-permute-start(f32[1,72,5184]{2,0,1:T(1,128)} %collective-permute-done.1), channel_id=1, source_target_pairs={{0,2},{2,4},{4,6},{6,8},{8,10},{10,12},{12,14},{14,16},{16,18},{18... | collective-permute-start | bytes 4478984 | tf_op jit(solution)/shard_map/ppermute | solution.py:18
  107.7 2.7 copy-start.6
  110.5 15.4 %copy-start.2 = (f32[1,72,5184]{2,1,0:T(8,128)}, f32[1,72,5184]{2,1,0:T(8,128)S(1)}, u32[]{:S(2)}) copy-start(f32[1,72,5184]{2,1,0:T(8,128)S(1)} %copy.144) | copy-start | bytes 4478980
  110.5 15.4 %copy-start = (f32[2,72,5184]{2,0,1:T(2,128)S(1)}, f32[2,72,5184]{2,0,1:T(2,128)}, u32[]{:S(2)}) copy-start(f32[2,72,5184]{2,0,1:T(2,128)} %all-gather.2.cloned.1.call-done) | copy-start | bytes 8957956
  112.6 17.4 %copy-start.3 = (f32[1,72,5184]{2,1,0:T(8,128)}, f32[1,72,5184]{2,1,0:T(8,128)S(1)}, u32[]{:S(2)}) copy-start(f32[1,72,5184]{2,1,0:T(8,128)S(1)} %copy.143) | copy-start | bytes 4478980
  125.9 4.1 copy-start.4
  389.9 6.2 %copy-start.1 = (f32[2,72,5184]{2,0,1:T(2,128)S(1)}, f32[2,72,5184]{2,0,1:T(2,128)}, u32[]{:S(2)}) copy-start(f32[2,72,5184]{2,0,1:T(2,128)} %all-gather.2.cloned.1.call-done) | copy-start | bytes 8957956
  409.3 21.9 %collective-permute-start.3 = (f32[1,72,5184]{2,1,0:T(8,128)S(1)}, f32[1,72,5184]{2,1,0:T(8,128)S(1)}, u32[]{:S(2)}, u32[]{:S(2)}) collective-permute-start(f32[1,72,5184]{2,1,0:T(8,128)S(1)} %negate_bitcast_fusion), channel_id=1, source_target_pairs={{0,2},{2,4},{4,6},{6,8},{8,10},{10,12},{12,14},{14,16},{16,18},{18... | collective-permute-start | bytes 4478984 | tf_op jit(solution)/shard_map/ppermute | solution.py:18
  431.4 26.6 %collective-permute-start.4 = (f32[1,72,5184]{2,1,0:T(8,128)S(1)}, f32[1,72,5184]{2,1,0:T(8,128)S(1)}, u32[]{:S(2)}, u32[]{:S(2)}) collective-permute-start(f32[1,72,5184]{2,1,0:T(8,128)S(1)} %bitcast_add_fusion.1), channel_id=1, source_target_pairs={{0,2},{2,4},{4,6},{6,8},{8,10},{10,12},{12,14},{14,16},{16,18},{18... | collective-permute-start | bytes 4478984 | tf_op jit(solution)/shard_map/ppermute | solution.py:18
  458.1 19.2 %collective-permute-start.5 = (f32[1,72,5184]{2,1,0:T(8,128)S(1)}, f32[1,72,5184]{2,1,0:T(8,128)S(1)}, u32[]{:S(2)}, u32[]{:S(2)}) collective-permute-start(f32[1,72,5184]{2,1,0:T(8,128)S(1)} %bitcast_add_fusion), channel_id=1, source_target_pairs={{0,26},{2,28},{4,30},{6,0},{8,2},{10,4},{12,6},{14,8},{16,10},{18,... | collective-permute-start | bytes 4478984 | tf_op jit(solution)/shard_map/ppermute | solution.py:18
  480.9 0.7 copy-start.7
Sparse Core Ops, SparseCore 0:
  8.9 46.2 all-gather.1
  481.0 82.4 all-reduce.2
where the time goes:
time: 580 us; the launch traced here: 573 us
  waiting for transfers between devices  252 us (43%)
  matrix products  173 us (30%)
  local copies, waits for them, and re-layouts  126 us (22%)
  between operations  14.6 us (3%)
  other arithmetic  7.41 us (1%)
    ppermute x6, waiting for transfers between devices, shifted(): return lax.ppermute(value, axis, pairs)  123 us
    dot_general x9, matrix products, inverse_axis(): jnp.einsum('pmk,kr->prm', values, table, precision=lax.Precision.HIGHEST)  88.5 us
    dot_general x9, matrix products, forward_axis(): jnp.einsum('pmc,kc->pkm', values, table, precision=lax.Precision.HIGHEST)  84.4 us
    unnamed x3, waiting for transfers between devices  81.5 us
    reshape x9, local copies, waits for them, and re-layouts, coulomb_filter(): work = inverse_axis(work.reshape(pairs, count * count, count), table)  51.9 us
    all_gather x1, waiting for transfers between devices, local(): whole = lax.all_gather(bands, 'grid', axis=1, tiled=True)  47.8 us
    reshape x6, local copies, waits for them, and re-layouts, coulomb_filter(): work = forward_axis(work.reshape(pairs, count * count, count), table)  35.5 us
    another operation x3, local copies, waits for them, and re-layouts, coulomb_filter(): work = forward_axis(density.reshape(pairs, count * count, count), table)  18.8 us
  transfers between devices with their start and end apart: 8, of which 8 were waited for; matrix products, arithmetic and copies ran while one was open for 2% of the time, Pallas kernels for 0%

commit v1 on v0

v1 whole, which is shorter than its diff:
```python
import functools
import math

import jax
import jax.numpy as jnp
import numpy as np
from jax import lax
from jax.experimental import pallas as pl
from jax.experimental.pallas import tpu as pltpu
from jax.sharding import PartitionSpec as P

LANES = 128
SUB = 8
CHUNK = 36
spacing = 0.5167


def ceil_to(value, unit):
    return -(-value // unit) * unit


class Geometry:
    def __init__(self, count):
        self.count = count
        self.rows = count // 2
        self.full = self.rows // SUB
        self.rest = self.rows - self.full * SUB
        self.plane = count * count
        self.seg = ceil_to(self.plane, LANES)
        self.half = ceil_to(self.plane // 2, LANES)
        self.width = self.full * self.seg + self.half
        assert count % 2 == 0 and self.rest * 2 == SUB and count % SUB == 0 and count <= LANES
        self.positions = np.concatenate(
            [
                np.arange(self.full * SUB),
                self.full * SUB + np.arange(self.rest),
                self.rows + self.full * SUB + np.arange(self.rest),
                self.rows + np.arange(self.full * SUB),
            ]
        )


def table_of(count):
    index = np.arange(count)
    half = count // 2
    freq = np.where(index <= half, index, index - half)
    phase = (freq[:, None] * index[None, :] % count) * (2.0 * math.pi / count)
    return np.where(index[:, None] <= half, np.cos(phase), np.sin(phase))


def split(table):
    high = table.astype(np.float32).astype(jnp.bfloat16).astype(np.float32)
    return high, (table - high).astype(np.float32)


def lane_weight(table):
    count = table.shape[0]
    high, low = split(table)
    weight = np.zeros((2 * LANES, 2 * LANES), np.float32)
    for part in range(2):
        weight[part * LANES : part * LANES + count, :count] = high
        weight[part * LANES : part * LANES + count, LANES : LANES + count] = low
    return weight


def row_weight(table):
    high, low = split(table)
    return np.concatenate([high, high, low], 1)


def dot(left, right):
    return jnp.dot(left, right, preferred_element_type=jnp.float32)


def residue(values):
    return values - values.astype(jnp.bfloat16).astype(jnp.float32)


def lane_stage(values, weight):
    both = dot(jnp.concatenate([values, residue(values)], 1), weight)
    return both[:, :LANES] + both[:, LANES:]


def row_stage(weight, values):
    return dot(weight, jnp.concatenate([values, residue(values), values], 0))


def frequency(index, half):
    return jnp.where(index <= half, index, index - half).astype(jnp.float32)


def weighting(index, half):
    return jnp.where((index == 0) | (index == half), 1.0, 2.0)


def fill_kernel(count, kernel_ref):
    half = count // 2
    factor = (2.0 * math.pi / (count * spacing)) ** 2

    def body(first, carry):
        second = lax.broadcasted_iota(jnp.int32, (count, LANES), 0)
        third = lax.broadcasted_iota(jnp.int32, (count, LANES), 1)
        ksq = factor * (
            frequency(first, half) ** 2 + frequency(second, half) ** 2 + frequency(third, half) ** 2
        )
        weights = weighting(first, half) * weighting(second, half) * weighting(third, half)
        value = weights * (-4.0 * math.pi / float(count**3)) / jnp.where(ksq > 0, ksq, 1.0)
        kernel_ref[pl.ds(first * count, count), :] = jnp.where((ksq > 0) & (third < count), value, 0.0)
        return carry

    lax.fori_loop(0, count, body, 0)


def pair_filter(count, home_ref, visit_ref, kernel_ref, weights, work, other, emit):
    w3, w1, w2, v2, v1, v3 = weights

    def pairs(ref, at):
        return jnp.concatenate([ref[pl.ds(at + k, count, stride=count), :] for k in range(2)], 1)

    def forward(i, carry):
        at = i * (CHUNK * count)
        density = home_ref[pl.ds(at, CHUNK * count), :] * visit_ref[pl.ds(at, CHUNK * count), :]
        lines = lane_stage(density, w3[...])
        for u in range(0, CHUNK, 2):
            cut = [lines[(u + k) * count : (u + k + 1) * count] for k in range(2)]
            out = row_stage(w1[...], jnp.concatenate(cut, 1))
            for k in range(2):
                work[pl.ds(at + (u + k) * count, count), :] = out[:, k * LANES : (k + 1) * LANES]
        return carry

    def middle(i, carry):
        for u in range(0, CHUNK, 2):
            q = i * CHUNK + u
            out = row_stage(w2[...], pairs(work, q))
            scale = [kernel_ref[pl.ds((q + k) * count, count), :] for k in range(2)]
            back = row_stage(v2[...], out * jnp.concatenate(scale, 1))
            for k in range(2):
                other[pl.ds((q + k) * count, count), :] = back[:, k * LANES : (k + 1) * LANES]
        return carry

    def inverse(i, carry):
        lines = []
        for u in range(0, CHUNK, 2):
            out = row_stage(v1[...], pairs(other, i * CHUNK + u))
            lines += [out[:, :LANES], out[:, LANES:]]
        emit(i * (CHUNK * count), CHUNK * count, lane_stage(jnp.concatenate(lines, 0), v3[...]))
        return carry

    for part in (forward, middle, inverse):
        lax.fori_loop(0, count // CHUNK, part, 0)


def slot_body(geo, first_ref, second_ref, visit_ref, *rest):
    weights = rest[:6]
    first_out, second_out, partner_m, partner_r, kernel_ref, work, other, partner = rest[6:]
    fill_kernel(geo.count, kernel_ref)
    for order, (home_ref, out_ref) in enumerate(((first_ref, first_out), (second_ref, second_out))):

        def emit(at, rows, potential):
            out_ref[pl.ds(at, rows), :] = potential * visit_ref[pl.ds(at, rows), :]
            term = potential * home_ref[pl.ds(at, rows), :]
            if order:
                term = term + partner[pl.ds(at, rows), :]
            partner[pl.ds(at, rows), :] = term

        pair_filter(geo.count, home_ref, visit_ref, kernel_ref, weights, work, other, emit)
    to_messages(geo, (partner,), partner_m, partner_r)


def lane_index(rows=SUB):
    return lax.broadcasted_iota(jnp.int32, (rows, LANES), 1)


def upper_rows():
    return lax.broadcasted_iota(jnp.int32, (SUB, LANES), 0) < SUB // 2


def swap_halves(values):
    return jnp.concatenate([values[SUB // 2 :], values[: SUB // 2]], 0)


def cut_lines(tiles, lines, count, put):
    lane = lane_index()
    for j in range(lines):
        tile, shift = divmod(j * count, LANES)
        value = tiles(tile)
        if shift:
            value = pltpu.roll(value, LANES - shift, 1)
        if shift + count > LANES:
            value = jnp.where(lane < LANES - shift, value, pltpu.roll(tiles(tile + 1), LANES - shift, 1))
        put(j, jnp.where(lane < count, value, 0.0))


def join_lines(line, lines, count, put):
    lane = lane_index()
    for tile in range(-(-lines * count // LANES)):
        low = tile * LANES
        value = None
        for j in range(low // count, min(lines, -(-(low + LANES) // count))):
            shift = j * count - low
            piece = line(j)
            if shift % LANES:
                piece = pltpu.roll(piece, shift % LANES, 1)
            value = piece if value is None else jnp.where(lane < shift, value, piece)
        put(tile, value)


def from_messages(geo, mains, others, band_ref):
    count, seg = geo.count, geo.seg

    def read(refs, at):
        value = refs[0][:, pl.ds(at, LANES)]
        for ref in refs[1:]:
            value = value + ref[:, pl.ds(at, LANES)]
        return value

    for refs, base in ((mains, 0), (others, (geo.full + 1) * SUB)):

        def body(i, carry):
            def put(j, value):
                band_ref[pl.ds(pl.multiple_of(j * count + base + i * SUB, SUB), SUB), :] = value

            cut_lines(lambda tile: read(refs, pl.multiple_of(i * seg + tile * LANES, LANES)), count, count, put)
            return carry

        lax.fori_loop(0, geo.full, body, 0)
    at = geo.full * seg
    held = {}
    cut_lines(lambda tile: read(mains, at + tile * LANES), count // 2, count, lambda j, value: held.update({j: value}))

    def put(j, value):
        main = held.pop(j)
        low = j * count + geo.full * SUB
        high = (j + count // 2) * count + geo.full * SUB
        band_ref[low : low + SUB, :] = jnp.where(upper_rows(), main, swap_halves(value))
        band_ref[high : high + SUB, :] = jnp.where(upper_rows(), swap_halves(main), value)

    cut_lines(lambda tile: read(others, at + tile * LANES), count // 2, count, put)


def to_messages(geo, bands, main_ref, other_ref):
    count, seg = geo.count, geo.seg

    def read(at):
        value = bands[0][pl.ds(at, SUB), :]
        for ref in bands[1:]:
            value = value + ref[pl.ds(at, SUB), :]
        return value

    for ref, base in ((main_ref, 0), (other_ref, (geo.full + 1) * SUB)):

        def body(i, carry):
            def put(tile, value):
                ref[:, pl.ds(pl.multiple_of(i * seg + tile * LANES, LANES), LANES)] = value

            join_lines(lambda j: read(pl.multiple_of(j * count + base + i * SUB, SUB)), count, count, put)
            return carry

        lax.fori_loop(0, geo.full, body, 0)
    at = geo.full * seg

    def line(j, main):
        low = read(j * count + geo.full * SUB)
        high = read((j + count // 2) * count + geo.full * SUB)
        if main:
            return jnp.where(upper_rows(), low, swap_halves(high))
        return jnp.where(upper_rows(), swap_halves(low), high)

    for ref, main in ((main_ref, True), (other_ref, False)):

        def put(tile, value):
            ref[:, at + tile * LANES : at + (tile + 1) * LANES] = value

        join_lines(lambda j: line(j, main), count // 2, count, put)


def pack_body(geo, bands_ref, mine_ref, other_ref):
    grid = lax.axis_index("grid")
    for ref, band in ((mine_ref, grid), (other_ref, 1 - grid)):
        for i in range(geo.full):
            ref[:, i * geo.seg : i * geo.seg + geo.plane] = bands_ref[band, i * SUB : (i + 1) * SUB, :]
        at = geo.full * geo.seg
        low = bands_ref[band, geo.full * SUB :, : geo.plane // 2]
        high = bands_ref[band, geo.full * SUB :, geo.plane // 2 :]
        ref[:, at : at + geo.plane // 2] = jnp.concatenate([low, high], 0)


def finish_body(geo, mine_count, *refs):
    out_ref = refs[-1]
    mines, others = refs[:mine_count], refs[mine_count:-1]
    grid = lax.axis_index("grid")
    for parts, band in ((mines, grid), (others, 1 - grid)):

        def total(low, high):
            value = parts[0][:, low:high]
            for ref in parts[1:]:
                value = value + ref[:, low:high]
            return value

        for i in range(geo.full):
            out_ref[band, i * SUB : (i + 1) * SUB, :] = total(i * geo.seg, i * geo.seg + geo.plane)
        at = geo.full * geo.seg
        rest = total(at, at + geo.plane // 2)
        out_ref[band, geo.full * SUB :, : geo.plane // 2] = rest[: SUB // 2]
        out_ref[band, geo.full * SUB :, geo.plane // 2 :] = rest[SUB // 2 :]


def call(body, name, inputs, outputs, scratch=(), micros=2):
    whole = pl.BlockSpec(memory_space=pltpu.VMEM)
    return pl.pallas_call(
        body,
        out_shape=[jax.ShapeDtypeStruct(shape, jnp.float32) for shape in outputs],
        in_specs=[whole] * len(inputs),
        out_specs=[whole] * len(outputs),
        scratch_shapes=[pltpu.VMEM(shape, jnp.float32) for shape in scratch],
        compiler_params=pltpu.CompilerParams(vmem_limit_bytes=56 * 2**20),
        cost_estimate=pl.CostEstimate(
            flops=int(micros * 3e8), bytes_accessed=int(micros * 1e6), transcendentals=0
        ),
        name=name,
    )(*inputs)


def local(bands):
    rows, plane = bands.shape[1:]
    count = rows * lax.axis_size("grid")
    assert bands.shape[0] == lax.axis_size("grid") == 2 and plane == count * count
    geo = Geometry(count)
    devices = lax.axis_size("band")
    assert devices % 2 == 0
    grid = lax.axis_index("grid")
    message = (SUB, geo.width)
    band = (plane, LANES)

    def move(value, pairs):
        return lax.ppermute(value, "band", [(i % devices, j % devices) for i, j in pairs])

    def swap(value):
        return lax.ppermute(value, "grid", [(0, 1), (1, 0)])

    even = range(0, devices, 2)
    odd = range(1, devices, 2)
    across = [(i, i + 1) for i in even]
    back = [(i, i - 1) for i in odd]

    table = table_of(count)
    order = geo.positions
    both = np.stack([table[:, order], table[:, (order + rows) % count]])
    first = jnp.where(grid == 0, row_weight(both[0]), row_weight(both[1]))
    last = jnp.where(grid == 0, row_weight(both[0].T), row_weight(both[1].T))
    weights = [
        jnp.asarray(lane_weight(table.T)),
        first,
        jnp.asarray(row_weight(table)),
        jnp.asarray(row_weight(table.T)),
        last,
        jnp.asarray(lane_weight(table)),
    ]

    mine, other = call(functools.partial(pack_body, geo), "pack", [bands], [message] * 2)

    def entry(part):
        z = move(part, [(i, i + 3) for i in odd] + across)
        x = move(part, [(i, i + 1) for i in odd])
        y = move(part, [(i, i + 2) for i in even])
        return {"x": (x, move(x, across)), "y": (y, move(y, across)), "z": (z,)}

    def unpack(mains, others):
        def body(*refs):
            from_messages(geo, refs[: len(mains)], refs[len(mains) : -1], refs[-1])

        return call(body, "unpack", [*mains, *others], [band])[0]

    rest_mine = swap(other)
    rest_other = swap(mine)
    own_entry = entry(mine)
    rest_entry = entry(rest_mine)
    home_mine = unpack((mine,), (rest_mine,))
    home_other = unpack((other,), (rest_other,))
    slots = {}
    for name in ("x", "y", "z"):
        visit = unpack(own_entry[name], rest_entry[name])
        slots[name] = call(
            functools.partial(slot_body, geo),
            "slot",
            [home_other, home_mine, visit, *weights],
            [band, band, message, message],
            [band] * 4,
            micros=20,
        )

    def sum_bands(index):
        def body(*refs):
            to_messages(geo, refs[:3], refs[3], refs[4])

        return call(body, "join", [slots[name][index] for name in ("x", "y", "z")], [message] * 2)

    other_m, other_r = sum_bands(0)
    mine_m, mine_r = sum_bands(1)
    returned = []
    for part in (2, 3):
        x, y, z = (slots[name][part] for name in ("x", "y", "z"))
        back_x = move(x + move(x, back), [(i, i - 1) for i in even])
        back_y = move(y + move(y, back), [(i, i - 2) for i in even])
        back_z = move(z, [(i, i - 3) for i in even] + back)
        returned.append((back_x, back_y, back_z))
    from_other = swap(other_r)
    from_mine = swap(mine_r + returned[1][0] + returned[1][1] + returned[1][2])
    parts = [mine_m, *returned[0], from_other, other_m, from_mine]
    return call(functools.partial(finish_body, geo, 5), "finish", parts, [bands.shape])[0]


def solution(mesh):
    return jax.shard_map(
        local,
        mesh=mesh,
        in_specs=(P("band", "grid", None),),
        out_specs=P("band", "grid", None),
        check_vma=False,
    )
```

time: 580 us -> 224 us (0.39); the launches traced: 573 us -> 223 us
  waiting for transfers between devices: 252 us -> 57.7 us
  matrix products: 173 us -> 0 us
  local copies, waits for them, and re-layouts: 126 us -> 10.5 us
  Pallas kernels: 0 us -> 105 us
  starting transfers between devices: 0.28 us -> 47 us
  between operations: 14.6 us -> 0.33 us
    dot_general x18 -> x0, matrix products: 173 us -> none  [the longest x9 88.5 us: inverse_axis(): jnp.einsum('pmk,kr->prm', values, table, precision=lax.Precision.HIGHEST)]
    pallas_call x0 -> x12, Pallas kernels: none -> 105 us  [call(): pl.pallas_call(body, out_shape=[jax.ShapeDtypeStruct(shape, jnp.float32)...]
    reshape x15 -> x0, local copies, waits for them, and re-layouts: 87.4 us -> none  [the longest x9 51.9 us: coulomb_filter(): work = inverse_axis(work.reshape(pairs, count * count, count), table)]
    unnamed x3 -> x0, waiting for transfers between devices: 81.5 us -> none
    ppermute x6 -> x24, waiting for transfers between devices: 123 us -> 57.7 us  [the longest x20 38 us: move(): lax.ppermute(value, 'band', [(i % devices, j % devices) for i, j in pairs])]
    all_gather x1 -> x0, waiting for transfers between devices: 47.8 us -> none  [local(): whole = lax.all_gather(bands, 'grid', axis=1, tiled=True)]
    ppermute x6 -> x24, starting transfers between devices: 0.24 us -> 47 us  [the longest x20 39.2 us: move(): lax.ppermute(value, 'band', [(i % devices, j % devices) for i, j in pairs])]
    another operation x3 -> x0, local copies, waits for them, and re-layouts: 18.8 us -> none  [coulomb_filter(): work = forward_axis(density.reshape(pairs, count * count, count), table)]
  transfers between devices with their start and end apart: 8 -> 24, of which waited for: 8 -> 10; matrix products, arithmetic and copies ran while one was open for 2% -> 1% of each run, Pallas kernels for 0% -> 44%
where the time goes in v1:
time: 224 us; the launch traced here: 223 us
  Pallas kernels  105 us (47%)
  waiting for transfers between devices  57.7 us (26%)
  starting transfers between devices  47 us (21%)
  local copies, waits for them, and re-layouts  10.5 us (5%)
  other arithmetic  2.38 us (1%)
    pallas_call x12, Pallas kernels, call(): pl.pallas_call(body, out_shape=[jax.ShapeDtypeStruct(shape, jnp.float32)...  105 us
    ppermute x20, starting transfers between devices, move(): lax.ppermute(value, 'band', [(i % devices, j % devices) for i, j in pairs])  39.2 us
    ppermute x20, waiting for transfers between devices, move(): lax.ppermute(value, 'band', [(i % devices, j % devices) for i, j in pairs])  38 us
    ppermute x4, waiting for transfers between devices, swap(): return lax.ppermute(value, 'grid', [(0, 1), (1, 0)])  19.7 us
    ppermute x4, starting transfers between devices, swap(): return lax.ppermute(value, 'grid', [(0, 1), (1, 0)])  7.81 us
    unnamed x47, local copies, waits for them, and re-layouts  7.16 us
  transfers between devices with their start and end apart: 24, of which 10 were waited for; matrix products, arithmetic and copies ran while one was open for 1% of the time, Pallas kernels for 44%

profile of v1, /device:TPU:0, one launch (start us, length us, event | category | flops | bytes accessed | tf_op | source)
XLA Modules:
  0.0 223.1 jit_solution(1604967861914410380)
XLA Ops:
  8.5 3.4 %collective-permute-start.6 = (f32[8,23680]{1,0:T(8,128)}, f32[8,23680]{1,0:T(8,128)}, u32[]{:S(2)}, u32[]{:S(2)}) collective-permute-start(f32[8,23680]{1,0:T(8,128)} %get-tuple-element.24.refs_0_), channel_id=1, source_target_pairs={{0,4},{4,8},{8,12},{12,16},{16,20},{20,24},{24,28},{28,0},{1,5},{5... | collective-permute-start | bytes 2273288 | tf_op jit(solution)/shard_map/ppermute | solution.py:336
  11.9 13.7 %collective-permute-done.1.refs_1_ = f32[8,23680]{1,0:T(8,128)S(1)} collective-permute-done((f32[8,23680]{1,0:T(8,128)}, f32[8,23680]{1,0:T(8,128)S(1)}, u32[]{:S(2)}, u32[]{:S(2)}) %collective-permute-start.1) | collective-permute-done | bytes 757792 | tf_op jit(solution)/shard_map/ppermute | solution.py:339
  25.6 3.7 %collective-permute-start.8 = (f32[8,23680]{1,0:T(8,128)S(1)}, f32[8,23680]{1,0:T(8,128)}, u32[]{:S(2)}, u32[]{:S(2)}) collective-permute-start(f32[8,23680]{1,0:T(8,128)S(1)} %collective-permute-done.1.refs_1_), channel_id=1, source_target_pairs={{0,4},{4,8},{8,12},{12,16},{16,20},{20,24},{24,28},{28,0},{1,5},{5... | collective-permute-start | bytes 2273288 | tf_op jit(solution)/shard_map/ppermute | solution.py:336
  33.4 4.9 %collective-permute-start.7 = (f32[8,23680]{1,0:T(8,128)}, f32[8,23680]{1,0:T(8,128)}, u32[]{:S(2)}, u32[]{:S(2)}) collective-permute-start(f32[8,23680]{1,0:T(8,128)} %collective-permute-done.6.refs_0_), channel_id=1, source_target_pairs={{0,2},{4,6},{8,10},{12,14},{16,18},{20,22},{24,26},{28,30},{1,3},{... | collective-permute-start | bytes 2273288 | tf_op jit(solution)/shard_map/ppermute | solution.py:336
  38.3 8.6 %collective-permute-done.8.refs_2_ = f32[8,23680]{1,0:T(8,128)} collective-permute-done((f32[8,23680]{1,0:T(8,128)S(1)}, f32[8,23680]{1,0:T(8,128)}, u32[]{:S(2)}, u32[]{:S(2)}) %collective-permute-start.8) | collective-permute-done | bytes 757792 | tf_op jit(solution)/shard_map/ppermute | solution.py:336
  51.4 6.8 %collective-permute-done.4.refs_2_ = f32[8,23680]{1,0:T(8,128)S(1)} collective-permute-done((f32[8,23680]{1,0:T(8,128)S(1)}, f32[8,23680]{1,0:T(8,128)S(1)}, u32[]{:S(2)}, u32[]{:S(2)}) %collective-permute-start.4) | collective-permute-done | bytes 757792 | tf_op jit(solution)/shard_map/ppermute | solution.py:336
  60.3 4.5 %unpack.6.second_ref = f32[5184,128]{1,0:T(8,128)} custom-call(f32[8,23680]{1,0:T(8,128)} %get-tuple-element.24.refs_0_, f32[8,23680]{1,0:T(8,128)} %copy-done.1), custom_call_target="tpu_custom_call" | custom-call | flops 600000000 | bytes 2000000 | tf_op jit(solution)/shard_map/unpack/pallas_call | solution.py:310
  64.8 4.5 %unpack.5.first_ref = f32[5184,128]{1,0:T(8,128)} custom-call(f32[8,23680]{1,0:T(8,128)} %get-tuple-element.23.refs_0_, f32[8,23680]{1,0:T(8,128)} %collective-permute-done.refs_1_), custom_call_target="tpu_custom_call" | custom-call | flops 600000000 | bytes 2000000 | tf_op jit(solution)/shard_map/unpack/pallas_call | solution.py:310
  69.4 5.0 %unpack.8.visit_ref = f32[5184,128]{1,0:T(8,128)} custom-call(f32[8,23680]{1,0:T(8,128)} %collective-permute-done.6.refs_0_, f32[8,23680]{1,0:T(8,128)} %collective-permute-done.7.refs_1_, f32[8,23680]{1,0:T(8,128)} %collective-permute-done.8.refs_2_, f32[8,23680]{1,0:T(8,128)} %collective-permute-done.9.refs_3_), custom_call_target="tpu_custom_call" | custom-call | flops 600000000 | bytes 2000000 | tf_op jit(solution)/shard_map/unpack/pallas_call | solution.py:310
  74.4 21.2 %slot.4 = (f32[5184,128]{1,0:T(8,128)}, f32[5184,128]{1,0:T(8,128)}, f32[8,23680]{1,0:T(8,128)}, f32[8,23680]{1,0:T(8,128)}) custom-call(f32[5184,128]{1,0:T(8,128)} %unpack.5.first_ref, f32[5184,128]{1,0:T(8,128)} %unpack.6.second_ref, f32[5184,128]{1,0:T(8,128)} %unpack.8.visit_ref, f32[256,256]{1,0:T(8,128)} %constant.26.clone.rest_0_, ...), custom_call_target="tpu_custom_call" | custom-call | flops 6000000000 | bytes 20000000 | tf_op jit(solution)/shard_map/slot/pallas_call | solution.py:310
  98.8 4.9 %unpack.7.visit_ref = f32[5184,128]{1,0:T(8,128)} custom-call(f32[8,23680]{1,0:T(8,128)} %copy-done.4, f32[8,23680]{1,0:T(8,128)} %copy-done.9, f32[8,23680]{1,0:T(8,128)} %copy-done.6, f32[8,23680]{1,0:T(8,128)} %copy-done.13), custom_call_target="tpu_custom_call" | custom-call | flops 600000000 | bytes 2000000 | tf_op jit(solution)/shard_map/unpack/pallas_call | solution.py:310
  103.8 21.1 %slot.3 = (f32[5184,128]{1,0:T(8,128)}, f32[5184,128]{1,0:T(8,128)}, f32[8,23680]{1,0:T(8,128)}, f32[8,23680]{1,0:T(8,128)}) custom-call(f32[5184,128]{1,0:T(8,128)} %unpack.5.first_ref, f32[5184,128]{1,0:T(8,128)} %unpack.6.second_ref, f32[5184,128]{1,0:T(8,128)} %unpack.7.visit_ref, f32[256,256]{1,0:T(8,128)} %constant.26.clone.rest_0_, ...), custom_call_target="tpu_custom_call" | custom-call | flops 6000000000 | bytes 20000000 | tf_op jit(solution)/shard_map/slot/pallas_call | solution.py:310
  128.0 4.4 %unpack.9.visit_ref = f32[5184,128]{1,0:T(8,128)} custom-call(f32[8,23680]{1,0:T(8,128)} %copy-done.11, f32[8,23680]{1,0:T(8,128)} %copy-done.14), custom_call_target="tpu_custom_call" | custom-call | flops 600000000 | bytes 2000000 | tf_op jit(solution)/shard_map/unpack/pallas_call | solution.py:310
  134.1 20.9 %slot.5 = (f32[5184,128]{1,0:T(8,128)}, f32[5184,128]{1,0:T(8,128)}, f32[8,23680]{1,0:T(8,128)}, f32[8,23680]{1,0:T(8,128)}) custom-call(f32[5184,128]{1,0:T(8,128)} %unpack.5.first_ref, f32[5184,128]{1,0:T(8,128)} %unpack.6.second_ref, f32[5184,128]{1,0:T(8,128)} %unpack.9.visit_ref, f32[256,256]{1,0:T(8,128)} %constant.26.clone.rest_0_, ...), custom_call_target="tpu_custom_call" | custom-call | flops 6000000000 | bytes 20000000 | tf_op jit(solution)/shard_map/slot/pallas_call | solution.py:310
  156.5 5.6 %collective-permute-start.22 = (f32[8,23680]{1,0:T(8,128)}, f32[8,23680]{1,0:T(8,128)S(1)}, u32[]{:S(2)}, u32[]{:S(2)}) collective-permute-start(f32[8,23680]{1,0:T(8,128)} %get-tuple-element.40), channel_id=1, source_target_pairs={{0,26},{4,30},{8,2},{12,6},{16,10},{20,14},{24,18},{28,22},{2,0},{... | collective-permute-start | bytes 2273288 | tf_op jit(solution)/shard_map/ppermute | solution.py:336
  166.9 6.0 %join.3 = (f32[8,23680]{1,0:T(8,128)}, f32[8,23680]{1,0:T(8,128)}) custom-call(f32[5184,128]{1,0:T(8,128)} %get-tuple-element.32.refs_0_, f32[5184,128]{1,0:T(8,128)} %get-tuple-element.33.refs_1_, f32[5184,128]{1,0:T(8,128)} %get-tuple-element.34.refs_2_), custom_call_target="tpu_custom_call" | custom-call | flops 600000000 | bytes 2000000 | tf_op jit(solution)/shard_map/join/pallas_call | solution.py:310
  172.9 6.0 %join.2 = (f32[8,23680]{1,0:T(8,128)}, f32[8,23680]{1,0:T(8,128)}) custom-call(f32[5184,128]{1,0:T(8,128)} %get-tuple-element.25.refs_0_, f32[5184,128]{1,0:T(8,128)} %get-tuple-element.26.refs_1_, f32[5184,128]{1,0:T(8,128)} %get-tuple-element.27.refs_2_), custom_call_target="tpu_custom_call" | custom-call | flops 600000000 | bytes 2000000 | tf_op jit(solution)/shard_map/join/pallas_call | solution.py:310
  180.7 3.3 %collective-permute-start.15 = (f32[8,23680]{1,0:T(8,128)S(1)}, f32[8,23680]{1,0:T(8,128)S(1)}, u32[]{:S(2)}, u32[]{:S(2)}) collective-permute-start(f32[8,23680]{1,0:T(8,128)S(1)} %add.22), channel_id=1, source_target_pairs={{0,28},{4,0},{8,4},{12,8},{16,12},{20,16},{24,20},{28,24},{1,29},{... | collective-permute-start | bytes 2273288 | tf_op jit(solution)/shard_map/ppermute | solution.py:336
  189.6 6.3 %collective-permute-done.16.refs_3_ = f32[8,23680]{1,0:T(8,128)S(1)} collective-permute-done((f32[8,23680]{1,0:T(8,128)}, f32[8,23680]{1,0:T(8,128)S(1)}, u32[]{:S(2)}, u32[]{:S(2)}) %collective-permute-start.16) | collective-permute-done | bytes 757792 | tf_op jit(solution)/shard_map/ppermute | solution.py:336
  196.0 3.2 %collective-permute-done.17.refs_4_ = f32[8,23680]{1,0:T(8,128)S(1)} collective-permute-done((f32[8,23680]{1,0:T(8,128)}, f32[8,23680]{1,0:T(8,128)S(1)}, u32[]{:S(2)}, u32[]{:S(2)}) %collective-permute-start.17) | collective-permute-done | bytes 757792 | tf_op jit(solution)/shard_map/ppermute | solution.py:339
  199.2 4.8 %collective-permute-done.15.refs_2_ = f32[8,23680]{1,0:T(8,128)S(1)} collective-permute-done((f32[8,23680]{1,0:T(8,128)S(1)}, f32[8,23680]{1,0:T(8,128)S(1)}, u32[]{:S(2)}, u32[]{:S(2)}) %collective-permute-start.15) | collective-permute-done | bytes 757792 | tf_op jit(solution)/shard_map/ppermute | solution.py:336
  204.0 8.1 %collective-permute-done.13.refs_1_ = f32[8,23680]{1,0:T(8,128)S(1)} collective-permute-done((f32[8,23680]{1,0:T(8,128)S(1)}, f32[8,23680]{1,0:T(8,128)S(1)}, u32[]{:S(2)}, u32[]{:S(2)}) %collective-permute-start.13) | collective-permute-done | bytes 757792 | tf_op jit(solution)/shard_map/ppermute | solution.py:336
  215.8 4.0 %finish.1 = f32[2,36,5184]{2,1,0:T(8,128)} custom-call(f32[8,23680]{1,0:T(8,128)} %get-tuple-element.28.refs_0_, f32[8,23680]{1,0:T(8,128)} %copy-done.17, f32[8,23680]{1,0:T(8,128)} %copy-done.16, f32[8,23680]{1,0:T(8,128)} %copy-done.8, f32[8,23680]{1,0:T(8,128)} %copy-done.12, f32[8,23680]{1,0:T(8,128)} %get-tuple-element.36.refs_5_, f32[8,23680]{1,0:T(8,128)} %copy-done.18), custom_call_target="tpu_custom_call" | custom-call | flops 600000000 | bytes 2000000 | tf_op jit(solution)/shard_map/finish/pallas_call | solution.py:310
  219.8 3.3 %copy.11 = f32[2,36,5184]{2,0,1:T(2,128)} copy(f32[2,36,5184]{2,1,0:T(8,128)} %finish.1) | data formatting | bytes 2985984 | tf_op jit(solution)/shard_map/finish/pallas_call | solution.py:310
  (90 shorter events, 44.4 us)
Async XLA Ops:
  5.5 20.1 %collective-permute-start.1 = (f32[8,23680]{1,0:T(8,128)}, f32[8,23680]{1,0:T(8,128)S(1)}, u32[]{:S(2)}, u32[]{:S(2)}) collective-permute-start(f32[8,23680]{1,0:T(8,128)} %get-tuple-element.23.refs_0_), channel_id=1, source_target_pairs={{0,1},{1,0},{2,3},{3,2},{4,5},{5,4},{6,7},{7,6},{8,9},{9,8},{10,11... | collective-permute-start | bytes 2273288 | tf_op jit(solution)/shard_map/ppermute | solution.py:339
  8.5 25.0 %collective-permute-start.6 = (f32[8,23680]{1,0:T(8,128)}, f32[8,23680]{1,0:T(8,128)}, u32[]{:S(2)}, u32[]{:S(2)}) collective-permute-start(f32[8,23680]{1,0:T(8,128)} %get-tuple-element.24.refs_0_), channel_id=1, source_target_pairs={{0,4},{4,8},{8,12},{12,16},{16,20},{20,24},{24,28},{28,0},{1,5},{5... | collective-permute-start | bytes 2273288 | tf_op jit(solution)/shard_map/ppermute | solution.py:336
  25.6 21.4 %collective-permute-start.8 = (f32[8,23680]{1,0:T(8,128)S(1)}, f32[8,23680]{1,0:T(8,128)}, u32[]{:S(2)}, u32[]{:S(2)}) collective-permute-start(f32[8,23680]{1,0:T(8,128)S(1)} %collective-permute-done.1.refs_1_), channel_id=1, source_target_pairs={{0,4},{4,8},{8,12},{12,16},{16,20},{20,24},{24,28},{28,0},{1,5},{5... | collective-permute-start | bytes 2273288 | tf_op jit(solution)/shard_map/ppermute | solution.py:336
  29.3 20.8 %collective-permute-start.2 = (f32[8,23680]{1,0:T(8,128)}, f32[8,23680]{1,0:T(8,128)S(1)}, u32[]{:S(2)}, u32[]{:S(2)}) collective-permute-start(f32[8,23680]{1,0:T(8,128)} %get-tuple-element.24.refs_0_), channel_id=1, source_target_pairs={{2,4},{6,8},{10,12},{14,16},{18,20},{22,24},{26,28},{30,0},{3,5},{... | collective-permute-start | bytes 2273288 | tf_op jit(solution)/shard_map/ppermute | solution.py:336
  30.6 27.6 %collective-permute-start.4 = (f32[8,23680]{1,0:T(8,128)S(1)}, f32[8,23680]{1,0:T(8,128)S(1)}, u32[]{:S(2)}, u32[]{:S(2)}) collective-permute-start(f32[8,23680]{1,0:T(8,128)S(1)} %collective-permute-done.1.refs_1_), channel_id=1, source_target_pairs={{2,4},{6,8},{10,12},{14,16},{18,20},{22,24},{26,28},{30,0},{3,5},{... | collective-permute-start | bytes 2273288 | tf_op jit(solution)/shard_map/ppermute | solution.py:336
  31.9 32.8 %collective-permute-start = (f32[8,23680]{1,0:T(8,128)}, f32[8,23680]{1,0:T(8,128)}, u32[]{:S(2)}, u32[]{:S(2)}) collective-permute-start(f32[8,23680]{1,0:T(8,128)} %get-tuple-element.24.refs_0_), channel_id=1, source_target_pairs={{0,1},{1,0},{2,3},{3,2},{4,5},{5,4},{6,7},{7,6},{8,9},{9,8},{10,11... | collective-permute-start | bytes 2273288 | tf_op jit(solution)/shard_map/ppermute | solution.py:339
  33.4 35.9 %collective-permute-start.7 = (f32[8,23680]{1,0:T(8,128)}, f32[8,23680]{1,0:T(8,128)}, u32[]{:S(2)}, u32[]{:S(2)}) collective-permute-start(f32[8,23680]{1,0:T(8,128)} %collective-permute-done.6.refs_0_), channel_id=1, source_target_pairs={{0,2},{4,6},{8,10},{12,14},{16,18},{20,22},{24,26},{28,30},{1,3},{... | collective-permute-start | bytes 2273288 | tf_op jit(solution)/shard_map/ppermute | solution.py:336
  47.0 22.4 %collective-permute-start.9 = (f32[8,23680]{1,0:T(8,128)}, f32[8,23680]{1,0:T(8,128)}, u32[]{:S(2)}, u32[]{:S(2)}) collective-permute-start(f32[8,23680]{1,0:T(8,128)} %collective-permute-done.8.refs_2_), channel_id=1, source_target_pairs={{0,2},{4,6},{8,10},{12,14},{16,18},{20,22},{24,26},{28,30},{1,3},{... | collective-permute-start | bytes 2273288 | tf_op jit(solution)/shard_map/ppermute | solution.py:336
  50.1 47.0 %collective-permute-start.3 = (f32[8,23680]{1,0:T(8,128)S(1)}, f32[8,23680]{1,0:T(8,128)S(1)}, u32[]{:S(2)}, u32[]{:S(2)}) collective-permute-start(f32[8,23680]{1,0:T(8,128)S(1)} %collective-permute-done.2.refs_0_), channel_id=1, source_target_pairs={{0,2},{4,6},{8,10},{12,14},{16,18},{20,22},{24,26},{28,30},{1,3},{... | collective-permute-start | bytes 2273288 | tf_op jit(solution)/shard_map/ppermute | solution.py:336
  58.2 38.9 %collective-permute-start.5 = (f32[8,23680]{1,0:T(8,128)S(1)}, f32[8,23680]{1,0:T(8,128)S(1)}, u32[]{:S(2)}, u32[]{:S(2)}) collective-permute-start(f32[8,23680]{1,0:T(8,128)S(1)} %collective-permute-done.4.refs_2_), channel_id=1, source_target_pairs={{0,2},{4,6},{8,10},{12,14},{16,18},{20,22},{24,26},{28,30},{1,3},{... | collective-permute-start | bytes 2273288 | tf_op jit(solution)/shard_map/ppermute | solution.py:336
  64.7 61.5 %collective-permute-start.10 = (f32[8,23680]{1,0:T(8,128)S(1)}, f32[8,23680]{1,0:T(8,128)S(1)}, u32[]{:S(2)}, u32[]{:S(2)}) collective-permute-start(f32[8,23680]{1,0:T(8,128)S(1)} %copy-done), channel_id=1, source_target_pairs={{2,8},{6,12},{10,16},{14,20},{18,24},{22,28},{26,0},{30,4},{0,2},{... | collective-permute-start | bytes 2273288 | tf_op jit(solution)/shard_map/ppermute | solution.py:336
  69.3 57.0 %collective-permute-start.11 = (f32[8,23680]{1,0:T(8,128)S(1)}, f32[8,23680]{1,0:T(8,128)S(1)}, u32[]{:S(2)}, u32[]{:S(2)}) collective-permute-start(f32[8,23680]{1,0:T(8,128)S(1)} %copy-done.2), channel_id=1, source_target_pairs={{2,8},{6,12},{10,16},{14,20},{18,24},{22,28},{26,0},{30,4},{0,2},{... | collective-permute-start | bytes 2273288 | tf_op jit(solution)/shard_map/ppermute | solution.py:336
  95.6 66.5 %collective-permute-start.20 = (f32[8,23680]{1,0:T(8,128)}, f32[8,23680]{1,0:T(8,128)S(1)}, u32[]{:S(2)}, u32[]{:S(2)}) collective-permute-start(f32[8,23680]{1,0:T(8,128)} %get-tuple-element.39), channel_id=1, source_target_pairs={{2,0},{6,4},{10,8},{14,12},{18,16},{22,20},{26,24},{30,28},{3,1},{... | collective-permute-start | bytes 2273288 | tf_op jit(solution)/shard_map/ppermute | solution.py:336
  124.8 39.5 %collective-permute-start.18 = (f32[8,23680]{1,0:T(8,128)}, f32[8,23680]{1,0:T(8,128)}, u32[]{:S(2)}, u32[]{:S(2)}) collective-permute-start(f32[8,23680]{1,0:T(8,128)} %get-tuple-element.38), channel_id=1, source_target_pairs={{2,0},{6,4},{10,8},{14,12},{18,16},{22,20},{26,24},{30,28},{3,1},{... | collective-permute-start | bytes 2273288 | tf_op jit(solution)/shard_map/ppermute | solution.py:336
  132.5 46.5 %collective-permute-start.14 = (f32[8,23680]{1,0:T(8,128)S(1)}, f32[8,23680]{1,0:T(8,128)S(1)}, u32[]{:S(2)}, u32[]{:S(2)}) collective-permute-start(f32[8,23680]{1,0:T(8,128)S(1)} %copy-done.3), channel_id=1, source_target_pairs={{2,0},{6,4},{10,8},{14,12},{18,16},{22,20},{26,24},{30,28},{3,1},{... | collective-permute-start | bytes 2273288 | tf_op jit(solution)/shard_map/ppermute | solution.py:336
  155.0 24.0 %collective-permute-start.12 = (f32[8,23680]{1,0:T(8,128)S(1)}, f32[8,23680]{1,0:T(8,128)S(1)}, u32[]{:S(2)}, u32[]{:S(2)}) collective-permute-start(f32[8,23680]{1,0:T(8,128)S(1)} %copy-done.5), channel_id=1, source_target_pairs={{2,0},{6,4},{10,8},{14,12},{18,16},{22,20},{26,24},{30,28},{3,1},{... | collective-permute-start | bytes 2273288 | tf_op jit(solution)/shard_map/ppermute | solution.py:336
  156.5 24.3 %collective-permute-start.22 = (f32[8,23680]{1,0:T(8,128)}, f32[8,23680]{1,0:T(8,128)S(1)}, u32[]{:S(2)}, u32[]{:S(2)}) collective-permute-start(f32[8,23680]{1,0:T(8,128)} %get-tuple-element.40), channel_id=1, source_target_pairs={{0,26},{4,30},{8,2},{12,6},{16,10},{20,14},{24,18},{28,22},{2,0},{... | collective-permute-start | bytes 2273288 | tf_op jit(solution)/shard_map/ppermute | solution.py:336
  162.2 21.9 %collective-permute-start.21 = (f32[8,23680]{1,0:T(8,128)S(1)}, f32[8,23680]{1,0:T(8,128)S(1)}, u32[]{:S(2)}, u32[]{:S(2)}) collective-permute-start(f32[8,23680]{1,0:T(8,128)S(1)} %add.25), channel_id=1, source_target_pairs={{0,28},{4,0},{8,4},{12,8},{16,12},{20,16},{24,20},{28,24},{1,29},{... | collective-permute-start | bytes 2273288 | tf_op jit(solution)/shard_map/ppermute | solution.py:336
  165.6 22.2 %collective-permute-start.19 = (f32[8,23680]{1,0:T(8,128)S(1)}, f32[8,23680]{1,0:T(8,128)S(1)}, u32[]{:S(2)}, u32[]{:S(2)}) collective-permute-start(f32[8,23680]{1,0:T(8,128)S(1)} %add.23), channel_id=1, source_target_pairs={{0,30},{4,2},{8,6},{12,10},{16,14},{20,18},{24,22},{28,26},{1,31},... | collective-permute-start | bytes 2273288 | tf_op jit(solution)/shard_map/ppermute | solution.py:336
  179.0 17.0 %collective-permute-start.16 = (f32[8,23680]{1,0:T(8,128)}, f32[8,23680]{1,0:T(8,128)S(1)}, u32[]{:S(2)}, u32[]{:S(2)}) collective-permute-start(f32[8,23680]{1,0:T(8,128)} %get-tuple-element.31), channel_id=1, source_target_pairs={{0,26},{4,30},{8,2},{12,6},{16,10},{20,14},{24,18},{28,22},{2,0},{... | collective-permute-start | bytes 2273288 | tf_op jit(solution)/shard_map/ppermute | solution.py:336
  179.1 20.1 %collective-permute-start.17 = (f32[8,23680]{1,0:T(8,128)}, f32[8,23680]{1,0:T(8,128)S(1)}, u32[]{:S(2)}, u32[]{:S(2)}) collective-permute-start(f32[8,23680]{1,0:T(8,128)} %get-tuple-element.35), channel_id=1, source_target_pairs={{0,1},{1,0},{2,3},{3,2},{4,5},{5,4},{6,7},{7,6},{8,9},{9,8},{10,11... | collective-permute-start | bytes 2273288 | tf_op jit(solution)/shard_map/ppermute | solution.py:339
  180.7 23.2 %collective-permute-start.15 = (f32[8,23680]{1,0:T(8,128)S(1)}, f32[8,23680]{1,0:T(8,128)S(1)}, u32[]{:S(2)}, u32[]{:S(2)}) collective-permute-start(f32[8,23680]{1,0:T(8,128)S(1)} %add.22), channel_id=1, source_target_pairs={{0,28},{4,0},{8,4},{12,8},{16,12},{20,16},{24,20},{28,24},{1,29},{... | collective-permute-start | bytes 2273288 | tf_op jit(solution)/shard_map/ppermute | solution.py:336
  184.1 28.0 %collective-permute-start.13 = (f32[8,23680]{1,0:T(8,128)S(1)}, f32[8,23680]{1,0:T(8,128)S(1)}, u32[]{:S(2)}, u32[]{:S(2)}) collective-permute-start(f32[8,23680]{1,0:T(8,128)S(1)} %add.21), channel_id=1, source_target_pairs={{0,30},{4,2},{8,6},{12,10},{16,14},{20,18},{24,22},{28,26},{1,31},... | collective-permute-start | bytes 2273288 | tf_op jit(solution)/shard_map/ppermute | solution.py:336
  187.9 27.0 %collective-permute-start.23 = (f32[8,23680]{1,0:T(8,128)S(1)}, f32[8,23680]{1,0:T(8,128)S(1)}, u32[]{:S(2)}, u32[]{:S(2)}) collective-permute-start(f32[8,23680]{1,0:T(8,128)S(1)} %add_add_fusion), channel_id=1, source_target_pairs={{0,1},{1,0},{2,3},{3,2},{4,5},{5,4},{6,7},{7,6},{8,9},{9,8},{10,11... | collective-permute-start | bytes 2273288 | tf_op jit(solution)/shard_map/ppermute | solution.py:339
  (23 other events, 497.9 us)
